TPU v7x, 32 devices: a whole 2x2x4 slice. The times are simulated.
32 devices in a mesh: heads: 2 (over x), cp: 16 (over z, y, core).
Axes of the slice: x: 2, y: 2, z: 4, core: 2. Of those that a mesh axis runs over, the one named last changes fastest.
Arguments:
- queries: bfloat16 [12, 128, 52, 128], P(None, 'cp', 'heads'), parts along dimension 2
- key_vecs: bfloat16 [2048, 52, 128], P('cp', 'heads'), parts along dimension 1
- value_vecs: bfloat16 [2048, 52, 128], P('cp', 'heads'), parts along dimension 1
- attn_out: bfloat16 [12, 128, 52, 128], P(None, 'cp', 'heads'), parts along dimension 2
- log_sum_exp: float32 [12, 128, 52], P(None, 'cp', 'heads'), parts along dimension 2
- grad_out: bfloat16 [12, 128, 52, 128], P(None, 'cp', 'heads'), parts along dimension 2
Outputs:
- output 1: bfloat16 [12, 128, 52, 128], P(None, 'cp', 'heads'), parts along dimension 2
- output 2: float32 [2048, 52, 128], P('cp', 'heads'), parts along dimension 1
- output 3: float32 [2048, 52, 128], P('cp', 'heads'), parts along dimension 1
There are 2 independent parts. A program takes and returns all parts, laid end to end along the dimension named above; each array names one.
All inputs are finite; a program needn't handle non-finite values.
Results may differ from a plain program's by a relative error of at most 0.001.
Values are sent between devices in bfloat16 or wider.
A program may use at most 1 GiB of HBM per device.

v0:
```python
import jax
import jax.numpy as jnp
from jax import lax
from jax.sharding import PartitionSpec as P


def tile_backward(q_tile, do_tile, lse_rows, delta_rows, key_tile, value_tile, q_start, k_start, score_scale):
    q_pos = q_start + jnp.arange(q_tile.shape[0])
    k_pos = k_start + jnp.arange(key_tile.shape[0])
    causal = (q_pos[:, None] >= k_pos[None, :])[None]
    scores = jnp.einsum("qhd,khd->hqk", q_tile, key_tile, preferred_element_type=jnp.float32) * score_scale
    weights = jnp.where(causal, jnp.exp(scores - lse_rows[:, :, None]), 0.0)
    part_v = jnp.einsum("hqk,qhd->khd", weights.astype(jnp.bfloat16), do_tile, preferred_element_type=jnp.float32)
    grad_p = jnp.einsum("qhd,khd->hqk", do_tile, value_tile, preferred_element_type=jnp.float32)
    grad_s = (weights * (grad_p - delta_rows[:, :, None])).astype(jnp.bfloat16)
    part_q = jnp.einsum("hqk,khd->qhd", grad_s, key_tile, preferred_element_type=jnp.float32)
    part_k = jnp.einsum("hqk,qhd->khd", grad_s, q_tile, preferred_element_type=jnp.float32) * score_scale
    return part_q, part_k, part_v


def solution(mesh):
    cp_size = mesh.shape["cp"]
    spec_q = P(None, "cp", "heads", None)
    spec_kv = P("cp", "heads", None)
    spec_lse = P(None, "cp", "heads")

    def per_device(queries, key_vecs, value_vecs, attn_out, log_sum_exp, grad_out):
        n_seg, q_local = queries.shape[:2]
        head_dim = queries.shape[3]
        key_local = key_vecs.shape[0]
        seg_len = q_local * cp_size
        prefix0 = key_local * cp_size - n_seg * seg_len
        score_scale = head_dim ** -0.5
        key_start = lax.axis_index("cp") * key_local
        source_offsets = q_local * jnp.arange(cp_size)
        row_delta = jnp.einsum("sqhd,sqhd->sqh", grad_out, attn_out, preferred_element_type=jnp.float32)

        def source_step(acc_pair, tile_in):
            acc_k, acc_v = acc_pair
            q_tile, do_tile, lse_tile, delta_tile, q_start = tile_in
            part_q, part_k, part_v = tile_backward(q_tile, do_tile, lse_tile.T, delta_tile.T, key_vecs, value_vecs, q_start, key_start, score_scale)
            return (acc_k + part_k, acc_v + part_v), part_q

        kv_acc = (jnp.zeros(key_vecs.shape, jnp.float32), jnp.zeros(value_vecs.shape, jnp.float32))
        dq_list = []
        for seg_idx in reversed(range(n_seg)):
            q_all = lax.all_gather(queries[seg_idx], "cp")
            do_all = lax.all_gather(grad_out[seg_idx], "cp")
            lse_all = lax.all_gather(log_sum_exp[seg_idx], "cp")
            delta_all = lax.all_gather(row_delta[seg_idx], "cp")
            q_starts = prefix0 + seg_idx * seg_len + source_offsets
            kv_acc, parts_q = lax.scan(source_step, kv_acc, (q_all, do_all, lse_all, delta_all, q_starts))
            dq_seg = lax.psum_scatter(parts_q, "cp", scatter_dimension=0) * score_scale
            dq_list.append(dq_seg.astype(jnp.bfloat16))
        return jnp.stack(dq_list[::-1]), kv_acc[0], kv_acc[1]

    return jax.shard_map(per_device, mesh=mesh, in_specs=(spec_q, spec_kv, spec_kv, spec_q, spec_lse, spec_q), out_specs=(spec_q, spec_kv, spec_kv), check_vma=False)
```

profile of v0, /device:TPU:0, one launch (start us, length us, event | category | flops | bytes accessed | tf_op | source)
XLA Modules:
  0.0 3805.1 jit_solution(14629427979766791640)
XLA Ops:
  15.7 25.6 all_gather.144
  42.1 20.1 all_gather.146
  63.4 18.7 all_gather.147
  82.8 17.8 all_gather.145
  101.9 188.9 %while.180 = (s32[]{:T(128)}, f32[128,26,128]{0,2,1:T(8,128)}, f32[128,26,128]{0,2,1:T(8,128)S(1)}, f32[16,8,26,128]{3,1,2,0:T(8,128)}, bf16[16,8,26,128]{3,1,2,...) while((s32[]{:T(128)}, f32[128,26,128]{0,2,1:T(8,128)}, ...), condition=%wide.region_1.2_spmd.clone, body=%wide.region_0.1_spmd.clone.sunk | while | flops 36396168 | bytes 10397572 | solution.py:52
  290.8 20.9 all_gather.148
  311.7 20.0 all_gather.150
  331.8 18.7 all_gather.151
  369.6 175.6 %while.169 = (s32[]{:T(128)}, f32[128,26,128]{0,2,1:T(8,128)}, f32[128,26,128]{0,2,1:T(8,128)S(1)}, f32[16,8,26,128]{3,1,2,0:T(8,128)}, bf16[16,8,26,128]{3,1,2,...) while((s32[]{:T(128)}, f32[128,26,128]{0,2,1:T(8,128)}, ...), condition=%wide.region_3.4_spmd, body=%wide.region_2.3_spmd.sunk | while | flops 35544200 | bytes 23816076 | solution.py:52
  545.2 20.9 all_gather.152
  566.1 20.0 all_gather.154
  586.1 18.7 all_gather.155
  624.0 171.5 %while.170 = (s32[]{:T(128)}, f32[128,26,128]{0,2,1:T(8,128)}, f32[128,26,128]{0,2,1:T(8,128)S(1)}, f32[16,8,26,128]{3,1,2,0:T(8,128)}, bf16[16,8,26,128]{3,1,2,...) while((s32[]{:T(128)}, f32[128,26,128]{0,2,1:T(8,128)}, ...), condition=%wide.region_5.6_spmd, body=%wide.region_4.5_spmd.sunk | while | flops 35544200 | bytes 23816076 | solution.py:52
  795.6 20.9 all_gather.156
  816.5 20.0 all_gather.158
  836.5 18.7 all_gather.159
  855.3 18.0 all_gather.157
  874.5 171.5 %while.171 = (s32[]{:T(128)}, f32[128,26,128]{0,2,1:T(8,128)}, f32[128,26,128]{0,2,1:T(8,128)S(1)}, f32[16,8,26,128]{3,1,2,0:T(8,128)}, bf16[16,8,26,128]{3,1,2,...) while((s32[]{:T(128)}, f32[128,26,128]{0,2,1:T(8,128)}, ...), condition=%wide.region_7.8_spmd, body=%wide.region_6.7_spmd.sunk | while | flops 35544200 | bytes 23816076 | solution.py:52
  1046.0 20.9 all_gather.160
  1066.9 20.0 all_gather.162
  1087.0 18.7 all_gather.163
  1124.8 174.7 %while.172 = (s32[]{:T(128)}, f32[128,26,128]{0,2,1:T(8,128)}, f32[128,26,128]{0,2,1:T(8,128)S(1)}, f32[16,8,26,128]{3,1,2,0:T(8,128)}, bf16[16,8,26,128]{3,1,2,...) while((s32[]{:T(128)}, f32[128,26,128]{0,2,1:T(8,128)}, ...), condition=%wide.region_9.10_spmd, body=%wide.region_8.9_spmd.sunk | while | flops 35544200 | bytes 23816076 | solution.py:52
  1299.5 20.9 all_gather.164
  1320.4 20.0 all_gather.166
  1340.5 18.7 all_gather.167
  1378.3 175.6 %while.173 = (s32[]{:T(128)}, f32[128,26,128]{0,2,1:T(8,128)}, f32[128,26,128]{0,2,1:T(8,128)S(1)}, f32[16,8,26,128]{3,1,2,0:T(8,128)}, bf16[16,8,26,128]{3,1,2,...) while((s32[]{:T(128)}, f32[128,26,128]{0,2,1:T(8,128)}, ...), condition=%wide.region_11.12_spmd, body=%wide.region_10.11_spmd.sunk | while | flops 35544200 | bytes 23816076 | solution.py:52
  1554.0 20.9 all_gather.168
  1574.9 20.0 all_gather.170
  1594.9 18.7 all_gather.171
  1632.7 171.6 %while.174 = (s32[]{:T(128)}, f32[128,26,128]{0,2,1:T(8,128)}, f32[128,26,128]{0,2,1:T(8,128)S(1)}, f32[16,8,26,128]{3,1,2,0:T(8,128)}, bf16[16,8,26,128]{3,1,2,...) while((s32[]{:T(128)}, f32[128,26,128]{0,2,1:T(8,128)}, ...), condition=%wide.region_13.14_spmd, body=%wide.region_12.13_spmd.sunk | while | flops 35544200 | bytes 23816076 | solution.py:52
  1804.4 20.9 all_gather.172
  1825.3 20.0 all_gather.174
  1845.3 18.7 all_gather.175
  1864.1 18.0 all_gather.173
  1883.4 173.6 %while.175 = (s32[]{:T(128)}, f32[128,26,128]{0,2,1:T(8,128)}, f32[128,26,128]{0,2,1:T(8,128)S(1)}, f32[16,8,26,128]{3,1,2,0:T(8,128)}, bf16[16,8,26,128]{3,1,2,...) while((s32[]{:T(128)}, f32[128,26,128]{0,2,1:T(8,128)}, ...), condition=%wide.region_15.16_spmd, body=%wide.region_14.15_spmd.sunk | while | flops 35544200 | bytes 23816076 | solution.py:52
  2057.0 20.9 all_gather.176
  2077.9 20.0 all_gather.178
  2098.0 18.7 all_gather.179
  2135.8 175.6 %while.176 = (s32[]{:T(128)}, f32[128,26,128]{0,2,1:T(8,128)}, f32[128,26,128]{0,2,1:T(8,128)S(1)}, f32[16,8,26,128]{3,1,2,0:T(8,128)}, bf16[16,8,26,128]{3,1,2,...) while((s32[]{:T(128)}, f32[128,26,128]{0,2,1:T(8,128)}, ...), condition=%wide.region_17.18_spmd, body=%wide.region_16.17_spmd.sunk | while | flops 35544200 | bytes 23816076 | solution.py:52
  2311.4 20.9 all_gather.180
  2332.3 20.0 all_gather.182
  2352.3 18.7 all_gather.183
  2390.1 172.5 %while.177 = (s32[]{:T(128)}, f32[128,26,128]{0,2,1:T(8,128)}, f32[128,26,128]{0,2,1:T(8,128)S(1)}, f32[16,8,26,128]{3,1,2,0:T(8,128)}, bf16[16,8,26,128]{3,1,2,...) while((s32[]{:T(128)}, f32[128,26,128]{0,2,1:T(8,128)}, ...), condition=%wide.region_19.20_spmd, body=%wide.region_18.19_spmd.sunk | while | flops 35544200 | bytes 23816076 | solution.py:52
  2562.7 20.9 all_gather.184
  2583.6 20.0 all_gather.186
  2603.7 18.7 all_gather.187
  2641.5 162.9 %while.178 = (s32[]{:T(128)}, f32[128,26,128]{0,2,1:T(8,128)}, f32[128,26,128]{0,2,1:T(8,128)S(1)}, f32[16,8,26,128]{3,1,2,0:T(8,128)}, bf16[16,8,26,128]{3,1,2,...) while((s32[]{:T(128)}, f32[128,26,128]{0,2,1:T(8,128)}, ...), condition=%wide.region_21.22_spmd, body=%wide.region_20.21_spmd.sunk | while | flops 35544200 | bytes 23816076 | solution.py:52
  2804.4 20.9 all_gather.188
  2825.3 20.0 all_gather.190
  2845.4 18.7 all_gather.191
  2864.1 18.0 all_gather.189
  2883.4 162.9 %while.179 = (s32[]{:T(128)}, f32[128,26,128]{0,2,1:T(8,128)}, f32[128,26,128]{0,2,1:T(8,128)S(1)}, f32[16,8,26,128]{3,1,2,0:T(8,128)}, bf16[16,8,26,128]{3,1,2,...) while((s32[]{:T(128)}, f32[128,26,128]{0,2,1:T(8,128)}, ...), condition=%wide.region_23.24_spmd, body=%wide.region_22.23_spmd.sunk | while | flops 35544200 | bytes 23816076 | solution.py:52
  3058.0 46.8 %reduce-scatter.13.cloned.1.call-done = f32[1,8,26,128]{3,1,2,0:T(8,128)} async-done(((f32[16,8,26,128]{3,1,2,0:T(8,128)}), f32[1,8,26,128]{3,1,2,0:T(8,128)}) %reduce-scatter.13.cloned.1.call-update) | async-done | bytes 106512 | tf_op jit(solution)/shard_map/reduce_scatter | solution.py:53
  3105.8 62.0 %reduce-scatter.15.cloned.1.call-done = f32[1,8,26,128]{3,1,2,0:T(8,128)} async-done(((f32[16,8,26,128]{3,1,2,0:T(8,128)}), f32[1,8,26,128]{3,1,2,0:T(8,128)}) %reduce-scatter.15.cloned.1.call-update) | async-done | bytes 106512 | tf_op jit(solution)/shard_map/reduce_scatter | solution.py:53
  3168.7 62.0 %reduce-scatter.17.cloned.1.call-done = f32[1,8,26,128]{3,1,2,0:T(8,128)} async-done(((f32[16,8,26,128]{3,1,2,0:T(8,128)}), f32[1,8,26,128]{3,1,2,0:T(8,128)}) %reduce-scatter.17.cloned.1.call-update) | async-done | bytes 106512 | tf_op jit(solution)/shard_map/reduce_scatter | solution.py:53
  3231.6 61.9 %reduce-scatter.19.cloned.1.call-done = f32[1,8,26,128]{3,1,2,0:T(8,128)} async-done(((f32[16,8,26,128]{3,1,2,0:T(8,128)}), f32[1,8,26,128]{3,1,2,0:T(8,128)}) %reduce-scatter.19.cloned.1.call-update) | async-done | bytes 106512 | tf_op jit(solution)/shard_map/reduce_scatter | solution.py:53
  3294.4 61.8 %reduce-scatter.21.cloned.1.call-done = f32[1,8,26,128]{3,1,2,0:T(8,128)} async-done(((f32[16,8,26,128]{3,1,2,0:T(8,128)}), f32[1,8,26,128]{3,1,2,0:T(8,128)}) %reduce-scatter.21.cloned.1.call-update) | async-done | bytes 106512 | tf_op jit(solution)/shard_map/reduce_scatter | solution.py:53
  3357.1 61.9 %reduce-scatter.23.cloned.1.call-done = f32[1,8,26,128]{3,1,2,0:T(8,128)} async-done(((f32[16,8,26,128]{3,1,2,0:T(8,128)}), f32[1,8,26,128]{3,1,2,0:T(8,128)}) %reduce-scatter.23.cloned.1.call-update) | async-done | bytes 106512 | tf_op jit(solution)/shard_map/reduce_scatter | solution.py:53
  3419.9 62.0 %reduce-scatter.25.cloned.1.call-done = f32[1,8,26,128]{3,1,2,0:T(8,128)} async-done(((f32[16,8,26,128]{3,1,2,0:T(8,128)}), f32[1,8,26,128]{3,1,2,0:T(8,128)}) %reduce-scatter.25.cloned.1.call-update) | async-done | bytes 106512 | tf_op jit(solution)/shard_map/reduce_scatter | solution.py:53
  3482.8 62.0 %reduce-scatter.27.cloned.1.call-done = f32[1,8,26,128]{3,1,2,0:T(8,128)} async-done(((f32[16,8,26,128]{3,1,2,0:T(8,128)}), f32[1,8,26,128]{3,1,2,0:T(8,128)}) %reduce-scatter.27.cloned.1.call-update) | async-done | bytes 106512 | tf_op jit(solution)/shard_map/reduce_scatter | solution.py:53
  3545.7 62.0 %reduce-scatter.29.cloned.1.call-done = f32[1,8,26,128]{3,1,2,0:T(8,128)} async-done(((f32[16,8,26,128]{3,1,2,0:T(8,128)}), f32[1,8,26,128]{3,1,2,0:T(8,128)}) %reduce-scatter.29.cloned.1.call-update) | async-done | bytes 106512 | tf_op jit(solution)/shard_map/reduce_scatter | solution.py:53
  3608.6 61.8 %reduce-scatter.31.cloned.1.call-done = f32[1,8,26,128]{3,1,2,0:T(8,128)} async-done(((f32[16,8,26,128]{3,1,2,0:T(8,128)}), f32[1,8,26,128]{3,1,2,0:T(8,128)}) %reduce-scatter.31.cloned.1.call-update) | async-done | bytes 106512 | tf_op jit(solution)/shard_map/reduce_scatter | solution.py:53
  3671.3 62.0 %reduce-scatter.33.cloned.1.call-done = f32[1,8,26,128]{3,1,2,0:T(8,128)} async-done(((f32[16,8,26,128]{3,1,2,0:T(8,128)}), f32[1,8,26,128]{3,1,2,0:T(8,128)}) %reduce-scatter.33.cloned.1.call-update) | async-done | bytes 106512 | tf_op jit(solution)/shard_map/reduce_scatter | solution.py:53
  3734.2 61.8 %reduce-scatter.35.cloned.1.call-done = f32[1,8,26,128]{3,1,2,0:T(8,128)} async-done(((f32[16,8,26,128]{3,1,2,0:T(8,128)}), f32[1,8,26,128]{3,1,2,0:T(8,128)}) %reduce-scatter.35.cloned.1.call-update) | async-done | bytes 106512 | tf_op jit(solution)/shard_map/reduce_scatter | solution.py:53
  (3187 shorter events, 2258.5 us)
Async XLA Ops:
  7.2 34.1 copy-start.25
  7.2 3097.7 %reduce-scatter.13.cloned.1.call-start = ((), (), s32[]{:S(2)}) async-start(), calls=%async_computation.12 | async-start | bytes 1810432 | tf_op jit(solution)/shard_map/reduce_scatter | solution.py:53
  15.6 46.6 %copy-start.26 = (bf16[12,8,26,128]{3,1,2,0:T(8,128)(2,1)S(1)}, bf16[12,8,26,128]{3,1,2,0:T(8,128)(2,1)}, u32[]{:S(2)}) copy-start(bf16[12,8,26,128]{3,1,2,0:T(8,128)(2,1)} %param.35) | copy-start | bytes 1916932
  15.6 46.6 %copy-start.27 = (bf16[12,8,26,128]{3,1,2,0:T(8,128)(2,1)S(1)}, bf16[12,8,26,128]{3,1,2,0:T(8,128)(2,1)}, u32[]{:S(2)}) copy-start(bf16[12,8,26,128]{3,1,2,0:T(8,128)(2,1)} %param.33) | copy-start | bytes 1916932
  42.1 40.0 %copy-start.38 = (f32[12,8,26]{2,1,0:T(8,128)S(1)}, f32[12,8,26]{2,1,0:T(8,128)}, u32[]{:S(2)}) copy-start(f32[12,8,26]{2,1,0:T(8,128)} %param.34) | copy-start | bytes 29956
  62.2 39.7 %copy-start = (bf16[128,26,128]{2,0,1:T(8,128)(2,1)S(1)}, bf16[128,26,128]{2,0,1:T(8,128)(2,1)}, u32[]{:S(2)}) copy-start(bf16[128,26,128]{2,0,1:T(8,128)(2,1)} %param.31) | copy-start | bytes 2555908
  62.2 39.7 %copy-start.23 = (bf16[128,26,128]{2,0,1:T(8,128)(2,1)S(1)}, bf16[128,26,128]{2,0,1:T(8,128)(2,1)}, u32[]{:S(2)}) copy-start(bf16[128,26,128]{2,0,1:T(8,128)(2,1)} %param.32) | copy-start | bytes 2555908
  108.0 2.5 copy-start.24
  119.2 3.2 copy-start.24
  131.0 3.2 copy-start.24
  142.9 3.2 copy-start.24
  154.7 3.2 copy-start.24
  166.6 3.2 copy-start.24
  178.5 3.2 copy-start.24
  190.3 3.2 copy-start.24
  202.1 3.2 copy-start.24
  214.0 3.2 copy-start.24
  225.9 3.2 copy-start.24
  237.7 3.2 copy-start.24
  249.6 3.2 copy-start.24
  261.4 3.2 copy-start.24
  273.3 3.2 copy-start.24
  285.1 3.2 copy-start.24
  290.8 40.9 %copy-start.37 = (f32[1,8,26]{1,2,0:T(8,128)S(1)}, f32[1,8,26]{1,2,0:T(8,128)}, u32[]{:S(2)}) copy-start(f32[1,8,26]{1,2,0:T(8,128)} %get-tuple-element.1342) | copy-start | bytes 2500
  290.8 59.7 %copy-start.48 = (f32[1,8,26]{2,1,0:T(8,128)S(1)}, f32[1,8,26]{2,1,0:T(8,128)}, u32[]{:S(2)}) copy-start(f32[1,8,26]{2,1,0:T(8,128)} %get-tuple-element.1353) | copy-start | bytes 2500
  545.1 40.9 %copy-start.36 = (f32[1,8,26]{1,2,0:T(8,128)S(1)}, f32[1,8,26]{1,2,0:T(8,128)}, u32[]{:S(2)}) copy-start(f32[1,8,26]{1,2,0:T(8,128)} %get-tuple-element.1341) | copy-start | bytes 2500
  545.2 59.7 %copy-start.47 = (f32[1,8,26]{2,1,0:T(8,128)S(1)}, f32[1,8,26]{2,1,0:T(8,128)}, u32[]{:S(2)}) copy-start(f32[1,8,26]{2,1,0:T(8,128)} %get-tuple-element.1352) | copy-start | bytes 2500
  795.6 40.9 %copy-start.35 = (f32[1,8,26]{1,2,0:T(8,128)S(1)}, f32[1,8,26]{1,2,0:T(8,128)}, u32[]{:S(2)}) copy-start(f32[1,8,26]{1,2,0:T(8,128)} %get-tuple-element.1340) | copy-start | bytes 2500
  795.6 59.7 %copy-start.46 = (f32[1,8,26]{2,1,0:T(8,128)S(1)}, f32[1,8,26]{2,1,0:T(8,128)}, u32[]{:S(2)}) copy-start(f32[1,8,26]{2,1,0:T(8,128)} %get-tuple-element.1351) | copy-start | bytes 2500
  1017.9 2.5 copy-start.5
  1046.0 40.9 %copy-start.34 = (f32[1,8,26]{1,2,0:T(8,128)S(1)}, f32[1,8,26]{1,2,0:T(8,128)}, u32[]{:S(2)}) copy-start(f32[1,8,26]{1,2,0:T(8,128)} %get-tuple-element.1339) | copy-start | bytes 2500
  1046.0 59.7 %copy-start.45 = (f32[1,8,26]{2,1,0:T(8,128)S(1)}, f32[1,8,26]{2,1,0:T(8,128)}, u32[]{:S(2)}) copy-start(f32[1,8,26]{2,1,0:T(8,128)} %get-tuple-element.1350) | copy-start | bytes 2500
  1227.3 2.5 copy-start.7
  1299.5 40.9 %copy-start.33 = (f32[1,8,26]{1,2,0:T(8,128)S(1)}, f32[1,8,26]{1,2,0:T(8,128)}, u32[]{:S(2)}) copy-start(f32[1,8,26]{1,2,0:T(8,128)} %get-tuple-element.1338) | copy-start | bytes 2500
  1299.5 59.7 %copy-start.44 = (f32[1,8,26]{2,1,0:T(8,128)S(1)}, f32[1,8,26]{2,1,0:T(8,128)}, u32[]{:S(2)}) copy-start(f32[1,8,26]{2,1,0:T(8,128)} %get-tuple-element.1349) | copy-start | bytes 2500
  1404.6 2.5 copy-start.9
  1553.9 40.9 %copy-start.32 = (f32[1,8,26]{1,2,0:T(8,128)S(1)}, f32[1,8,26]{1,2,0:T(8,128)}, u32[]{:S(2)}) copy-start(f32[1,8,26]{1,2,0:T(8,128)} %get-tuple-element.1337) | copy-start | bytes 2500
  1553.9 59.7 %copy-start.43 = (f32[1,8,26]{2,1,0:T(8,128)S(1)}, f32[1,8,26]{2,1,0:T(8,128)}, u32[]{:S(2)}) copy-start(f32[1,8,26]{2,1,0:T(8,128)} %get-tuple-element.1348) | copy-start | bytes 2500
  1679.7 2.5 copy-start.11
  1804.4 40.9 %copy-start.31 = (f32[1,8,26]{1,2,0:T(8,128)S(1)}, f32[1,8,26]{1,2,0:T(8,128)}, u32[]{:S(2)}) copy-start(f32[1,8,26]{1,2,0:T(8,128)} %get-tuple-element.1336) | copy-start | bytes 2500
  1804.4 59.7 %copy-start.42 = (f32[1,8,26]{2,1,0:T(8,128)S(1)}, f32[1,8,26]{2,1,0:T(8,128)}, u32[]{:S(2)}) copy-start(f32[1,8,26]{2,1,0:T(8,128)} %get-tuple-element.1347) | copy-start | bytes 2500
  1898.4 2.5 copy-start.13
  2028.6 2.5 copy-start.13
  2057.0 40.9 %copy-start.30 = (f32[1,8,26]{1,2,0:T(8,128)S(1)}, f32[1,8,26]{1,2,0:T(8,128)}, u32[]{:S(2)}) copy-start(f32[1,8,26]{1,2,0:T(8,128)} %get-tuple-element.1335) | copy-start | bytes 2500
  2057.0 59.7 %copy-start.41 = (f32[1,8,26]{2,1,0:T(8,128)S(1)}, f32[1,8,26]{2,1,0:T(8,128)}, u32[]{:S(2)}) copy-start(f32[1,8,26]{2,1,0:T(8,128)} %get-tuple-element.1346) | copy-start | bytes 2500
  2184.0 2.5 copy-start.15
  2562.7 40.9 %copy-start.29 = (f32[1,8,26]{1,2,0:T(8,128)S(1)}, f32[1,8,26]{1,2,0:T(8,128)}, u32[]{:S(2)}) copy-start(f32[1,8,26]{1,2,0:T(8,128)} %get-tuple-element.1333) | copy-start | bytes 2500
  2562.7 59.7 %copy-start.40 = (f32[1,8,26]{2,1,0:T(8,128)S(1)}, f32[1,8,26]{2,1,0:T(8,128)}, u32[]{:S(2)}) copy-start(f32[1,8,26]{2,1,0:T(8,128)} %get-tuple-element.1355) | copy-start | bytes 2500
  2562.7 78.8 %copy-start.51 = (s32[16]{0:T(128)S(1)}, s32[16]{0:T(128)}, u32[]{:S(2)}) copy-start(s32[16]{0:T(128)} %fusion.242) | copy-start | bytes 196
  2726.5 2.5 copy-start.19
  2804.4 40.9 %copy-start.28 = (f32[1,8,26]{1,2,0:T(8,128)S(1)}, f32[1,8,26]{1,2,0:T(8,128)}, u32[]{:S(2)}) copy-start(f32[1,8,26]{1,2,0:T(8,128)} %get-tuple-element.1332) | copy-start | bytes 2500
  2804.4 59.7 %copy-start.39 = (f32[1,8,26]{2,1,0:T(8,128)S(1)}, f32[1,8,26]{2,1,0:T(8,128)}, u32[]{:S(2)}) copy-start(f32[1,8,26]{2,1,0:T(8,128)} %get-tuple-element.1344) | copy-start | bytes 2500
  2804.4 79.0 %copy-start.50 = (s32[16]{0:T(128)S(1)}, s32[16]{0:T(128)}, u32[]{:S(2)}) copy-start(s32[16]{0:T(128)} %fusion.241) | copy-start | bytes 196
  3046.3 121.4 %reduce-scatter.15.cloned.1.call-start = ((), (), s32[]{:S(2)}) async-start(), calls=%async_computation.13 | async-start | bytes 1810432 | tf_op jit(solution)/shard_map/reduce_scatter | solution.py:53
  3047.1 183.6 %reduce-scatter.17.cloned.1.call-start = ((), (), s32[]{:S(2)}) async-start(), calls=%async_computation.14 | async-start | bytes 1810432 | tf_op jit(solution)/shard_map/reduce_scatter | solution.py:53
  3047.8 245.6 %reduce-scatter.19.cloned.1.call-start = ((), (), s32[]{:S(2)}) async-start(), calls=%async_computation.15 | async-start | bytes 1810432 | tf_op jit(solution)/shard_map/reduce_scatter | solution.py:53
  3048.4 307.8 %reduce-scatter.21.cloned.1.call-start = ((), (), s32[]{:S(2)}) async-start(), calls=%async_computation.16 | async-start | bytes 1810432 | tf_op jit(solution)/shard_map/reduce_scatter | solution.py:53
  3049.0 370.0 %reduce-scatter.23.cloned.1.call-start = ((), (), s32[]{:S(2)}) async-start(), calls=%async_computation.17 | async-start | bytes 1810432 | tf_op jit(solution)/shard_map/reduce_scatter | solution.py:53
  3049.6 432.3 %reduce-scatter.25.cloned.1.call-start = ((), (), s32[]{:S(2)}) async-start(), calls=%async_computation.18 | async-start | bytes 1810432 | tf_op jit(solution)/shard_map/reduce_scatter | solution.py:53
  3050.3 494.4 %reduce-scatter.27.cloned.1.call-start = ((), (), s32[]{:S(2)}) async-start(), calls=%async_computation.19 | async-start | bytes 1810432 | tf_op jit(solution)/shard_map/reduce_scatter | solution.py:53
  3051.1 556.6 %reduce-scatter.29.cloned.1.call-start = ((), (), s32[]{:S(2)}) async-start(), calls=%async_computation.20 | async-start | bytes 1810432 | tf_op jit(solution)/shard_map/reduce_scatter | solution.py:53
  3051.8 618.6 %reduce-scatter.31.cloned.1.call-start = ((), (), s32[]{:S(2)}) async-start(), calls=%async_computation.21 | async-start | bytes 1810432 | tf_op jit(solution)/shard_map/reduce_scatter | solution.py:53
  3052.4 680.9 %reduce-scatter.33.cloned.1.call-start = ((), (), s32[]{:S(2)}) async-start(), calls=%async_computation.22 | async-start | bytes 1810432 | tf_op jit(solution)/shard_map/reduce_scatter | solution.py:53
  3053.1 742.9 %reduce-scatter.35.cloned.1.call-start = ((), (), s32[]{:S(2)}) async-start(), calls=%async_computation.23 | async-start | bytes 1810432 | tf_op jit(solution)/shard_map/reduce_scatter | solution.py:53
  (345 other events, 630.1 us)
Sparse Core Ops, SparseCore 0:
  3046.5 58.3 reduce-scatter.12
  3108.5 59.1 reduce-scatter.14
  3171.5 59.1 reduce-scatter.16
  3234.2 59.1 reduce-scatter.18
  3297.0 59.1 reduce-scatter.20
  3359.7 59.1 reduce-scatter.22
  3422.7 59.1 reduce-scatter.24
  3485.5 59.1 reduce-scatter.26
  3548.4 59.1 reduce-scatter.28
  3611.2 59.1 reduce-scatter.30
  3674.0 59.2 reduce-scatter.32
  3736.8 59.1 reduce-scatter.34
where the time goes:
time: 3860 us; the launch traced here: 3810 us
  matrix products  1330 us (34%)
  blocking collectives  934 us (24%)
  waiting for transfers between devices  735 us (19%)
  local copies, waits for them, and re-layouts  620 us (16%)
  other arithmetic  155 us (4%)
    reduce_scatter x12, waiting for transfers between devices, per_device(): dq_seg = lax.psum_scatter(parts_q, 'cp', scatter_dimension=0) * score_scale  728 us
    dynamic_slice x768, local copies, waits for them, and re-layouts, per_device(): lax.scan(source_step, kv_acc, (q_all, do_all, lse_all, delta_all, q_starts))  385 us
    dot_general x192, matrix products, tile_backward(): jnp.einsum('hqk,qhd->khd', grad_s, q_tile, preferred_element_type=jnp.flo...  303 us
    dot_general x192, matrix products, tile_backward(): jnp.einsum('qhd,khd->hqk', do_tile, value_tile, preferred_element_type=jn...  296 us
    dot_general x192, matrix products, tile_backward(): jnp.einsum('hqk,qhd->khd', weights.astype(jnp.bfloat16), do_tile, preferr...  286 us
    dot_general x192, matrix products, tile_backward(): jnp.einsum('qhd,khd->hqk', q_tile, key_tile, preferred_element_type=jnp.f...  257 us
    all_gather x12, blocking collectives, per_device(): q_all = lax.all_gather(queries[seg_idx], 'cp')  256 us
    all_gather x12, blocking collectives, per_device(): do_all = lax.all_gather(grad_out[seg_idx], 'cp')  240 us
  transfers between devices with their start and end apart: 12, of which 12 were waited for; matrix products, arithmetic and copies ran while one was open for 0% of the time, Pallas kernels for 0%

commit v1 on v0

v1 whole, which is shorter than its diff:
```python
import functools

import jax
import jax.numpy as jnp
from jax import lax
from jax.experimental import pallas as pl
from jax.experimental.pallas import tpu as pltpu
from jax.sharding import PartitionSpec as P

MESH = pl.DeviceIdType.MESH
N_CP = 16
N_HEADS = 26
N_SLOTS = 2
N_GROUPS = 3
G_ROWS = 32
SEG_PER_G = 4
Q_LOCAL = 8
K_LOCAL = 128
HD = 128
SEG_LEN = N_CP * Q_LOCAL
GROUP_Q = N_CP * G_ROWS
KEY_SUPER = 512
SRC_PER_SUPER = KEY_SUPER // K_LOCAL
N_SUPER = N_CP // SRC_PER_SUPER
PREFIX0 = 512
KEY_TILE = 256


def head_of(slot, dev):
    second = jnp.where(dev % 2 == 0, 16 + dev // 2, jnp.where(dev == 5, 24, 25))
    return jnp.where(slot == 0, dev, second)


def slots_of(dev):
    return jnp.where((dev % 2 == 0) | (dev == 5) | (dev == 11), 2, 1)


def kernel(qd_ref, kv_ref, st_ref, dq_out, dkv_out, q_buf, kv_buf, st_buf, dq_acc, dq_stage, dkv_stage, in_sems, send_sems, ret_sems, out_sems):
    me = lax.axis_index("cp")
    my_slots = slots_of(me)
    score_scale = HD ** -0.5

    barrier = pltpu.get_barrier_semaphore()

    def greet(k, carry):
        pl.semaphore_signal(barrier, inc=1, device_id={"cp": lax.rem(me + k, N_CP)}, device_id_type=MESH)
        return carry

    lax.fori_loop(1, N_CP, greet, 0)
    pl.semaphore_wait(barrier, N_CP - 1)

    def in_parts(slot, head, src):
        return (
            (qd_ref.at[head], q_buf.at[slot, :, :, src]),
            (kv_ref.at[head], kv_buf.at[slot, :, src]),
            (st_ref.at[head], st_buf.at[slot, src]),
        )

    def in_copies(slot, dev):
        head = head_of(slot, dev)
        return [
            pltpu.make_async_remote_copy(
                src_ref=src, dst_ref=dst, send_sem=send_sems.at[slot, kind, dev], recv_sem=in_sems.at[slot, kind],
                device_id={"cp": dev}, device_id_type=MESH,
            )
            for kind, (src, dst) in enumerate(in_parts(slot, head, me))
        ]

    for slot in range(N_SLOTS):

        @pl.when(slot < my_slots)
        def _():
            for kind, (src, dst) in enumerate(in_parts(slot, head_of(slot, me), me)):
                pltpu.make_async_copy(src, dst, in_sems.at[slot, kind]).start()

        def send(k, carry):
            dev = lax.rem(me + k, N_CP)

            @pl.when(slot < slots_of(dev))
            def _():
                for copy in in_copies(slot, dev):
                    copy.start()

            return carry

        lax.fori_loop(1, N_CP, send, 0)

    def dkv_remote(slot, dev):
        return pltpu.make_async_remote_copy(
            src_ref=dkv_stage.at[slot, :, dev], dst_ref=dkv_out.at[head_of(slot, me)], send_sem=ret_sems.at[slot, 1, dev],
            recv_sem=out_sems.at[1], device_id={"cp": dev}, device_id_type=MESH,
        )

    def dq_remote(slot, dev):
        return pltpu.make_async_remote_copy(
            src_ref=dq_stage.at[slot, :, dev], dst_ref=dq_out.at[head_of(slot, me)], send_sem=ret_sems.at[slot, 0, dev],
            recv_sem=out_sems.at[0], device_id={"cp": dev}, device_id_type=MESH,
        )

    key_iota = lax.broadcasted_iota(jnp.int32, (KEY_TILE, GROUP_Q), 0)
    lane = lax.broadcasted_iota(jnp.int32, (1, GROUP_Q), 1)
    lane_pos = PREFIX0 + (lane % G_ROWS // Q_LOCAL) * SEG_LEN + (lane // G_ROWS) * Q_LOCAL + lane % Q_LOCAL

    def run_slot(slot, carry):
        for kind, buf in enumerate((q_buf, kv_buf, st_buf)):
            pltpu.make_async_copy(buf.at[slot], buf.at[slot], in_sems.at[slot, kind]).wait()
        dq_acc[...] = jnp.zeros_like(dq_acc)

        def run_super(sup, carry):
            dkv_stage[slot, :, pl.ds(sup * SRC_PER_SUPER, SRC_PER_SUPER)] = jnp.zeros((2, SRC_PER_SUPER, K_LOCAL, HD), jnp.float32)

            def run_group(grp, carry):
                q = q_buf[slot, 0, grp].reshape(GROUP_Q, HD)
                do = q_buf[slot, 1, grp].reshape(GROUP_Q, HD)
                lse_rows, delta_rows = [], []
                for quad in range(N_CP // 4):
                    lse_rows.append(jnp.sum(st_buf[slot, pl.ds(quad * 4, 4), grp], axis=0, keepdims=True))
                    delta_rows.append(jnp.sum(st_buf[slot, pl.ds(quad * 4, 4), N_GROUPS + grp], axis=0, keepdims=True))
                lse = jnp.concatenate(lse_rows, axis=1)
                delta = jnp.concatenate(delta_rows, axis=1)
                q_pos = lane_pos + grp * (SEG_PER_G * SEG_LEN)
                dq_part = jnp.zeros((GROUP_Q, HD), jnp.float32)
                for tile in range(KEY_SUPER // KEY_TILE):
                    per = KEY_TILE // K_LOCAL
                    block = pl.ds(sup * SRC_PER_SUPER + tile * per, per)
                    key = kv_buf[slot, 0, block].reshape(KEY_TILE, HD)
                    val = kv_buf[slot, 1, block].reshape(KEY_TILE, HD)
                    causal = key_iota + (sup * KEY_SUPER + tile * KEY_TILE) <= q_pos
                    contract_last = (((1,), (1,)), ((), ()))
                    scores = lax.dot_general(key, q, contract_last, preferred_element_type=jnp.float32) * score_scale
                    weights = jnp.where(causal, jnp.exp(scores - lse), 0.0)
                    grad_p = lax.dot_general(val, do, contract_last, preferred_element_type=jnp.float32)
                    grad_s = (weights * (grad_p - delta)).astype(jnp.bfloat16)
                    part_v = jnp.dot(weights.astype(jnp.bfloat16), do, preferred_element_type=jnp.float32)
                    part_k = jnp.dot(grad_s, q, preferred_element_type=jnp.float32)
                    dkv_stage[slot, 0, block] += (part_k * score_scale).reshape(per, K_LOCAL, HD)
                    dkv_stage[slot, 1, block] += part_v.reshape(per, K_LOCAL, HD)
                    dq_part += lax.dot_general(grad_s, key, (((0,), (0,)), ((), ())), preferred_element_type=jnp.float32)
                dq_acc[grp] += dq_part
                return carry

            lax.fori_loop(jnp.maximum(sup - 1, 0), N_GROUPS, run_group, 0)

            def give_back(k, carry):
                dev = sup * SRC_PER_SUPER + k

                @pl.when(dev != me)
                def _():
                    dkv_remote(slot, dev).start()

                @pl.when(dev == me)
                def _():
                    pltpu.make_async_copy(dkv_stage.at[slot, :, me], dkv_out.at[head_of(slot, me)], out_sems.at[1]).start()

                return carry

            lax.fori_loop(0, SRC_PER_SUPER, give_back, 0)
            return carry

        lax.fori_loop(0, N_SUPER, run_super, 0)
        dq_stage[slot] = (dq_acc[...] * score_scale).astype(jnp.bfloat16).reshape(N_GROUPS, N_CP, G_ROWS, HD)
        pltpu.make_async_copy(dq_stage.at[slot, :, me], dq_out.at[head_of(slot, me)], out_sems.at[0]).start()

        def give_dq(k, carry):
            dq_remote(slot, lax.rem(me + k, N_CP)).start()
            return carry

        lax.fori_loop(1, N_CP, give_dq, 0)
        return carry

    lax.fori_loop(0, my_slots, run_slot, 0)

    pltpu.make_async_copy(dq_out, dq_out, out_sems.at[0]).wait()
    pltpu.make_async_copy(dkv_out, dkv_out, out_sems.at[1]).wait()

    for slot in range(N_SLOTS):

        def drain(k, carry):
            dev = lax.rem(me + k, N_CP)

            @pl.when(slot < slots_of(dev))
            def _():
                for copy in in_copies(slot, dev):
                    copy.wait_send()

            @pl.when(slot < my_slots)
            def _():
                dq_remote(slot, dev).wait_send()
                dkv_remote(slot, dev).wait_send()

            return carry

        lax.fori_loop(1, N_CP, drain, 0)


def solution(mesh):
    spec_q = P(None, "cp", "heads", None)
    spec_kv = P("cp", "heads", None)
    spec_lse = P(None, "cp", "heads")

    def per_device(queries, key_vecs, value_vecs, attn_out, log_sum_exp, grad_out):
        rows = queries.shape[0] * queries.shape[1]
        row_delta = jnp.sum(grad_out.astype(jnp.float32) * attn_out.astype(jnp.float32), axis=-1)
        by_head = lambda x: x.reshape(rows, N_HEADS, HD).transpose(1, 0, 2).reshape(N_HEADS, N_GROUPS, G_ROWS, HD)
        qd = jnp.stack([by_head(queries), by_head(grad_out)], axis=1)
        kv = jnp.stack([key_vecs.transpose(1, 0, 2), value_vecs.transpose(1, 0, 2)], axis=1)
        stats = jnp.stack([log_sum_exp, row_delta]).reshape(2, N_GROUPS, G_ROWS, N_HEADS).transpose(3, 0, 1, 2).reshape(N_HEADS, 6, 1, G_ROWS)
        quarter = (jnp.arange(4) == lax.axis_index("cp") % 4)[:, None]
        stats = jnp.where(quarter, stats, 0.0).reshape(N_HEADS, 6, 4 * G_ROWS)
        stats = jnp.pad(stats, ((0, 0), (0, 2), (0, 0)))

        any_spec = pl.BlockSpec(memory_space=pl.ANY)
        dq, dkv = pl.pallas_call(
            kernel,
            out_shape=(
                jax.ShapeDtypeStruct((N_HEADS, N_GROUPS, G_ROWS, HD), jnp.bfloat16),
                jax.ShapeDtypeStruct((N_HEADS, 2, K_LOCAL, HD), jnp.float32),
            ),
            in_specs=[any_spec] * 3,
            out_specs=(any_spec, any_spec),
            scratch_shapes=[
                pltpu.VMEM((N_SLOTS, 2, N_GROUPS, N_CP, G_ROWS, HD), jnp.bfloat16),
                pltpu.VMEM((N_SLOTS, 2, N_CP, K_LOCAL, HD), jnp.bfloat16),
                pltpu.VMEM((N_SLOTS, N_CP, 8, 128), jnp.float32),
                pltpu.VMEM((N_GROUPS, GROUP_Q, HD), jnp.float32),
                pltpu.VMEM((N_SLOTS, N_GROUPS, N_CP, G_ROWS, HD), jnp.bfloat16),
                pltpu.VMEM((N_SLOTS, 2, N_CP, K_LOCAL, HD), jnp.float32),
                pltpu.SemaphoreType.DMA((N_SLOTS, 3)),
                pltpu.SemaphoreType.DMA((N_SLOTS, 3, N_CP)),
                pltpu.SemaphoreType.DMA((N_SLOTS, 2, N_CP)),
                pltpu.SemaphoreType.DMA((2,)),
            ],
            compiler_params=pltpu.CompilerParams(collective_id=0, has_side_effects=True, vmem_limit_bytes=40 * 1024 * 1024),
            name="head_exchange",
        )(qd, kv, stats)

        dq = dq.reshape(N_HEADS, rows, HD).transpose(1, 0, 2).reshape(queries.shape)
        return dq, dkv[:, 0].transpose(1, 0, 2), dkv[:, 1].transpose(1, 0, 2)

    return jax.shard_map(per_device, mesh=mesh, in_specs=(spec_q, spec_kv, spec_kv, spec_q, spec_lse, spec_q), out_specs=(spec_q, spec_kv, spec_kv), check_vma=False)
```

time: 3860 us -> 176 us (0.05); the launches traced: 3810 us -> 174 us
  matrix products: 1330 us -> 0 us
  blocking collectives: 934 us -> 0 us
  waiting for transfers between devices: 735 us -> 0 us
  local copies, waits for them, and re-layouts: 620 us -> 5.32 us
  Pallas kernels: 0 us -> 166 us
  other arithmetic: 155 us -> 2.04 us
    dot_general x960 -> x0, matrix products: 1330 us -> none  [the longest x192 303 us: tile_backward(): jnp.einsum('hqk,qhd->khd', grad_s, q_tile, preferred_element_type=jnp.flo...]
    all_gather x48 -> x0, blocking collectives: 934 us -> none  [the longest x12 256 us: per_device(): q_all = lax.all_gather(queries[seg_idx], 'cp')]
    reduce_scatter x12 -> x0, waiting for transfers between devices: 728 us -> none  [per_device(): dq_seg = lax.psum_scatter(parts_q, 'cp', scatter_dimension=0) * score_scale]
    dynamic_slice x768 -> x0, local copies, waits for them, and re-layouts: 385 us -> none  [per_device(): lax.scan(source_step, kv_acc, (q_all, do_all, lse_all, delta_all, q_starts))]
    while x736 -> x0, local copies, waits for them, and re-layouts: 208 us -> none
    pallas_call x0 -> x1, Pallas kernels: none -> 166 us  [per_device(): pl.pallas_call(kernel, out_shape=(jax.ShapeDtypeStruct((N_HEADS, N_GROUPS...]
    add x396 -> x0, other arithmetic: 130 us -> none  [the longest x192 123 us: tile_backward(): q_pos = q_start + jnp.arange(q_tile.shape[0])]
  transfers between devices with their start and end apart: 12 -> 0, of which waited for: 12 -> 0; matrix products, arithmetic and copies ran while one was open for 0% -> 0% of each run, Pallas kernels for 0% -> 0%
where the time goes in v1:
time: 176 us; the launch traced here: 174 us
  Pallas kernels  166 us (94%)
  local copies, waits for them, and re-layouts  5.32 us (3%)
  other arithmetic  2.04 us (1%)
    pallas_call x1, Pallas kernels, per_device(): pl.pallas_call(kernel, out_shape=(jax.ShapeDtypeStruct((N_HEADS, N_GROUPS...  166 us

profile of v1, /device:TPU:0, one launch (start us, length us, event | category | flops | bytes accessed | tf_op | source)
XLA Modules:
  0.0 174.1 jit_solution(10843306022055470142)
XLA Ops:
  0.6 0.0 copy-start.4
  0.6 0.0 copy-start.3
  0.7 0.1 broadcast_in_dim.29
  0.7 0.1 broadcast_in_dim.30
  0.8 1.7 multiply_reduce_fusion
  2.5 0.0 copy-start
  2.5 0.1 copy.22
  2.7 0.0 copy-done.4
  2.7 0.1 copy.23
  2.8 0.1 broadcast_in_dim.33
  2.9 0.2 broadcast_in_dim.34
  3.1 0.1 copy_select_fusion
  3.2 0.0 copy-done.3
  3.2 0.1 copy.20
  3.3 0.3 copy-done
  3.6 0.0 copy-start.1
  3.6 0.0 copy-start.2
  3.6 0.1 copy.21
  3.7 0.1 pad_maximum_fusion.1.qd_ref
  3.9 0.9 copy-done.1
  4.8 0.3 copy-done.2
  5.0 0.2 pad_maximum_fusion.kv_ref
  5.2 166.0 %head_exchange.1 = (bf16[26,3,32,128]{3,2,1,0:T(8,128)(2,1)S(1)}, f32[26,2,128,128]{3,2,1,0:T(8,128)S(1)}) custom-call(bf16[26,2,3,32,128]{4,3,2,1,0:T(8,128)(2,1)S(1)} %pad_maximum_fusion.1.qd_ref, bf16[26,2,128,128]{3,2,1,0:T(8,128)(2,1)S(1)} %pad_maximum_fusion.kv_ref, f32[26,8,128]{2,1,0:T(8,128)S(1)} %pad.4.st_ref), custom_call_target="tpu_custom_call" | custom-call | tf_op jit(solution)/shard_map/head_exchange/pallas_call | solution.py:213
  171.2 0.9 copy.25
  172.1 2.0 %slice_bitcast_fusion = (f32[128,26,128]{2,0,1:T(8,128)}, f32[128,26,128]{2,0,1:T(8,128)}) fusion(f32[26,2,128,128]{3,2,1,0:T(8,128)S(1)} %get-tuple-element.6), kind=kLoop, calls=%fused_computation.1 | loop fusion | bytes 6815744 | tf_op jit(solution)/shard_map/transpose | solution.py:238
  (3 shorter events, 0.0 us)
Async XLA Ops:
  0.6 2.1 %copy-start.4 = (f32[12,8,26]{2,1,0:T(8,128)S(1)}, f32[12,8,26]{2,1,0:T(8,128)}, u32[]{:S(2)}) copy-start(f32[12,8,26]{2,1,0:T(8,128)} %param.10) | copy-start | bytes 29956
  0.6 2.5 %copy-start.3 = (bf16[12,8,26,128]{3,1,2,0:T(8,128)(2,1)S(1)}, bf16[12,8,26,128]{3,1,2,0:T(8,128)(2,1)}, u32[]{:S(2)}) copy-start(bf16[12,8,26,128]{3,1,2,0:T(8,128)(2,1)} %param.6) | copy-start | bytes 1916932
  2.5 1.1 copy-start
  3.6 1.2 copy-start.1
  3.6 1.4 copy-start.2

commit v2 on v1

v2 whole, which is shorter than its diff:
```python
import functools

import jax
import jax.numpy as jnp
from jax import lax
from jax.experimental import pallas as pl
from jax.experimental.pallas import tpu as pltpu
from jax.sharding import PartitionSpec as P

MESH = pl.DeviceIdType.MESH
N_CP = 16
N_HEADS = 26
N_HALF = 8
N_SLOTS = 5
N_GROUPS = 3
G_ROWS = 32
SEG_PER_G = 4
Q_LOCAL = 8
K_LOCAL = 128
HD = 128
SEG_LEN = N_CP * Q_LOCAL
GROUP_Q = N_CP * G_ROWS
KEY_SUPER = 512
SRC_PER_SUPER = KEY_SUPER // K_LOCAL
SUPER_PER_HALF = N_HALF // SRC_PER_SUPER
PREFIX0 = 512
KEY_TILE = 256


def at_end(dev):
    return (dev < 4) | (dev >= 12)


def head_of(slot, dev):
    return jnp.where(at_end(dev), 19 + 3 * slot, 4 * slot) + dev % 4


def slots_of(dev):
    pos = dev % 4
    return jnp.where(at_end(dev), jnp.where(pos >= 1, 2, 1), jnp.where(pos <= 2, 5, 4))


def kernel(qd_ref, kv_ref, st_ref, dq_out, dkv_out, q_buf, kv_buf, st_buf, part_buf, dq_acc, dq_stage, dkv_stage, in_sems, send_sems, ret_sems, part_sems, out_sems):
    me = lax.axis_index("cp")
    my_slots = slots_of(me)
    half = me // N_HALF
    half_dev = half * N_HALF
    partner = (3 - me // 4) * 4 + me % 4
    score_scale = HD ** -0.5

    barrier = pltpu.get_barrier_semaphore()

    def greet(k, carry):
        pl.semaphore_signal(barrier, inc=1, device_id={"cp": lax.rem(me + k, N_CP)}, device_id_type=MESH)
        return carry

    lax.fori_loop(1, N_CP, greet, 0)
    pl.semaphore_wait(barrier, N_CP - 1)

    def in_parts(slot, dev, dev_half):
        head = head_of(slot, dev)
        first = dev_half
        q_part = (0, qd_ref.at[head, :, first:], q_buf.at[slot, :, first:, me])
        kv_part = (1, kv_ref.at[head], kv_buf.at[slot, :, me % N_HALF])
        st_part = (2, st_ref.at[head], st_buf.at[slot, me])
        return q_part, kv_part, st_part

    def in_remote(slot, dev, part):
        kind, src, dst = part
        return pltpu.make_async_remote_copy(
            src_ref=src, dst_ref=dst, send_sem=send_sems.at[slot, kind, dev], recv_sem=in_sems.at[slot, kind],
            device_id={"cp": dev}, device_id_type=MESH,
        )

    def each_in_copy(slot, dev, act):
        for dev_half in range(2):

            @pl.when((slot < slots_of(dev)) & (dev // N_HALF == dev_half))
            def _():
                q_part, kv_part, st_part = in_parts(slot, dev, dev_half)
                act(in_remote(slot, dev, st_part))
                act(in_remote(slot, dev, q_part))

                @pl.when(half == dev_half)
                def _():
                    act(in_remote(slot, dev, kv_part))

    for slot in range(N_SLOTS):
        for my_half in range(2):

            @pl.when((slot < my_slots) & (half == my_half))
            def _():
                for kind, src, dst in in_parts(slot, me, my_half):
                    pltpu.make_async_copy(src, dst, in_sems.at[slot, kind]).start()

        def send(k, carry):
            each_in_copy(slot, lax.rem(me + k, N_CP), lambda copy: copy.start())
            return carry

        lax.fori_loop(1, N_CP, send, 0)

    def dkv_remote(slot, dev):
        return pltpu.make_async_remote_copy(
            src_ref=dkv_stage.at[slot, :, dev % N_HALF], dst_ref=dkv_out.at[head_of(slot, me)], send_sem=ret_sems.at[slot, 1, dev % N_HALF],
            recv_sem=out_sems.at[1], device_id={"cp": dev}, device_id_type=MESH,
        )

    def dq_remote(slot, dev):
        return pltpu.make_async_remote_copy(
            src_ref=dq_stage.at[slot, :, dev % N_HALF], dst_ref=dq_out.at[head_of(slot, me)], send_sem=ret_sems.at[slot, 0, dev % N_HALF],
            recv_sem=out_sems.at[0], device_id={"cp": dev}, device_id_type=MESH,
        )

    def part_remote(slot, my_half):
        first, other = my_half, (1 - my_half) * N_HALF
        return pltpu.make_async_remote_copy(
            src_ref=dq_acc.at[slot, first:, other:other + N_HALF], dst_ref=part_buf.at[slot, first:], send_sem=part_sems.at[0, slot],
            recv_sem=part_sems.at[1, slot], device_id={"cp": partner}, device_id_type=MESH,
        )

    key_iota = lax.broadcasted_iota(jnp.int32, (KEY_TILE, GROUP_Q), 0)
    lane = lax.broadcasted_iota(jnp.int32, (1, GROUP_Q), 1)
    lane_pos = PREFIX0 + (lane % G_ROWS // Q_LOCAL) * SEG_LEN + (lane // G_ROWS) * Q_LOCAL + lane % Q_LOCAL

    def finish_dq(slot):
        for my_half in range(2):

            @pl.when(half == my_half)
            def _():
                arrived = part_buf.at[slot, 1 - my_half:]
                pltpu.make_async_copy(arrived, arrived, part_sems.at[1, slot]).wait()
                own = pl.ds(my_half * N_HALF, N_HALF)
                first = dq_acc[slot, 0, own] if my_half == 0 else part_buf[slot, 0]
                dq_stage[slot, 0] = (first * score_scale).astype(jnp.bfloat16)
                for grp in range(1, N_GROUPS):
                    dq_stage[slot, grp] = ((dq_acc[slot, grp, own] + part_buf[slot, grp]) * score_scale).astype(jnp.bfloat16)

        pltpu.make_async_copy(dq_stage.at[slot, :, me % N_HALF], dq_out.at[head_of(slot, me)], out_sems.at[0]).start()

        def give_dq(k, carry):
            dq_remote(slot, half_dev + lax.rem(me + k, N_HALF)).start()
            return carry

        lax.fori_loop(1, N_HALF, give_dq, 0)

    def run_slot(slot, carry):
        for my_half in range(2):

            @pl.when(half == my_half)
            def _():
                arrived = q_buf.at[slot, :, my_half:]
                pltpu.make_async_copy(arrived, arrived, in_sems.at[slot, 0]).wait()

        for kind, buf in ((1, kv_buf), (2, st_buf)):
            pltpu.make_async_copy(buf.at[slot], buf.at[slot], in_sems.at[slot, kind]).wait()
        dq_acc[slot] = jnp.zeros(dq_acc.shape[1:], jnp.float32)

        def run_super(sup_local, carry):
            sup = half * SUPER_PER_HALF + sup_local
            dkv_stage[slot, :, pl.ds(sup_local * SRC_PER_SUPER, SRC_PER_SUPER)] = jnp.zeros((2, SRC_PER_SUPER, K_LOCAL, HD), jnp.float32)

            def run_group(grp, carry):
                q = q_buf[slot, 0, grp].reshape(GROUP_Q, HD)
                do = q_buf[slot, 1, grp].reshape(GROUP_Q, HD)
                lse_rows, delta_rows = [], []
                for quad in range(N_CP // 4):
                    lse_rows.append(jnp.sum(st_buf[slot, pl.ds(quad * 4, 4), grp], axis=0, keepdims=True))
                    delta_rows.append(jnp.sum(st_buf[slot, pl.ds(quad * 4, 4), N_GROUPS + grp], axis=0, keepdims=True))
                lse = jnp.concatenate(lse_rows, axis=1)
                delta = jnp.concatenate(delta_rows, axis=1)
                q_pos = lane_pos + grp * (SEG_PER_G * SEG_LEN)
                dq_part = jnp.zeros((GROUP_Q, HD), jnp.float32)
                for tile in range(KEY_SUPER // KEY_TILE):
                    per = KEY_TILE // K_LOCAL
                    block = pl.ds(sup_local * SRC_PER_SUPER + tile * per, per)
                    key = kv_buf[slot, 0, block].reshape(KEY_TILE, HD)
                    val = kv_buf[slot, 1, block].reshape(KEY_TILE, HD)
                    causal = key_iota + (sup * KEY_SUPER + tile * KEY_TILE) <= q_pos
                    contract_last = (((1,), (1,)), ((), ()))
                    scores = lax.dot_general(key, q, contract_last, preferred_element_type=jnp.float32) * score_scale
                    weights = jnp.where(causal, jnp.exp(scores - lse), 0.0)
                    grad_p = lax.dot_general(val, do, contract_last, preferred_element_type=jnp.float32)
                    grad_s = (weights * (grad_p - delta)).astype(jnp.bfloat16)
                    part_v = jnp.dot(weights.astype(jnp.bfloat16), do, preferred_element_type=jnp.float32)
                    part_k = jnp.dot(grad_s, q, preferred_element_type=jnp.float32)
                    dkv_stage[slot, 0, block] += (part_k * score_scale).reshape(per, K_LOCAL, HD)
                    dkv_stage[slot, 1, block] += part_v.reshape(per, K_LOCAL, HD)
                    dq_part += lax.dot_general(grad_s, key, (((0,), (0,)), ((), ())), preferred_element_type=jnp.float32)
                dq_acc[slot, grp] += dq_part.reshape(N_CP, G_ROWS, HD)
                return carry

            lax.fori_loop(jnp.maximum(sup - 1, 0), N_GROUPS, run_group, 0)

            def give_back(k, carry):
                dev = half_dev + sup_local * SRC_PER_SUPER + k

                @pl.when(dev != me)
                def _():
                    dkv_remote(slot, dev).start()

                @pl.when(dev == me)
                def _():
                    pltpu.make_async_copy(dkv_stage.at[slot, :, me % N_HALF], dkv_out.at[head_of(slot, me)], out_sems.at[1]).start()

                return carry

            lax.fori_loop(0, SRC_PER_SUPER, give_back, 0)
            return carry

        lax.fori_loop(0, SUPER_PER_HALF, run_super, 0)
        for my_half in range(2):

            @pl.when(half == my_half)
            def _():
                part_remote(slot, my_half).start()

        @pl.when(slot > 0)
        def _():
            finish_dq(slot - 1)

        return carry

    lax.fori_loop(0, my_slots, run_slot, 0)
    finish_dq(my_slots - 1)

    pltpu.make_async_copy(dq_out, dq_out, out_sems.at[0]).wait()
    pltpu.make_async_copy(dkv_out, dkv_out, out_sems.at[1]).wait()

    for slot in range(N_SLOTS):

        def drain(k, carry):
            each_in_copy(slot, lax.rem(me + k, N_CP), lambda copy: copy.wait_send())
            return carry

        lax.fori_loop(1, N_CP, drain, 0)

        @pl.when(slot < my_slots)
        def _():
            def drain_back(k, carry):
                dev = half_dev + lax.rem(me + k, N_HALF)
                dq_remote(slot, dev).wait_send()
                dkv_remote(slot, dev).wait_send()
                return carry

            lax.fori_loop(1, N_HALF, drain_back, 0)
            for my_half in range(2):

                @pl.when(half == my_half)
                def _():
                    part_remote(slot, my_half).wait_send()


def solution(mesh):
    spec_q = P(None, "cp", "heads", None)
    spec_kv = P("cp", "heads", None)
    spec_lse = P(None, "cp", "heads")

    def per_device(queries, key_vecs, value_vecs, attn_out, log_sum_exp, grad_out):
        rows = queries.shape[0] * queries.shape[1]
        row_delta = jnp.sum(grad_out.astype(jnp.float32) * attn_out.astype(jnp.float32), axis=-1)
        by_head = lambda x: x.reshape(rows, N_HEADS, HD).transpose(1, 0, 2).reshape(N_HEADS, N_GROUPS, G_ROWS, HD)
        qd = jnp.stack([by_head(queries), by_head(grad_out)], axis=1)
        kv = jnp.stack([key_vecs.transpose(1, 0, 2), value_vecs.transpose(1, 0, 2)], axis=1)
        stats = jnp.stack([log_sum_exp, row_delta]).reshape(2, N_GROUPS, G_ROWS, N_HEADS).transpose(3, 0, 1, 2).reshape(N_HEADS, 6, 1, G_ROWS)
        quarter = (jnp.arange(4) == lax.axis_index("cp") % 4)[:, None]
        stats = jnp.where(quarter, stats, 0.0).reshape(N_HEADS, 6, 4 * G_ROWS)
        stats = jnp.pad(stats, ((0, 0), (0, 2), (0, 0)))

        any_spec = pl.BlockSpec(memory_space=pl.ANY)
        dq, dkv = pl.pallas_call(
            kernel,
            out_shape=(
                jax.ShapeDtypeStruct((N_HEADS, N_GROUPS, G_ROWS, HD), jnp.bfloat16),
                jax.ShapeDtypeStruct((N_HEADS, 2, K_LOCAL, HD), jnp.float32),
            ),
            in_specs=[any_spec] * 3,
            out_specs=(any_spec, any_spec),
            scratch_shapes=[
                pltpu.VMEM((N_SLOTS, 2, N_GROUPS, N_CP, G_ROWS, HD), jnp.bfloat16),
                pltpu.VMEM((N_SLOTS, 2, N_HALF, K_LOCAL, HD), jnp.bfloat16),
                pltpu.VMEM((N_SLOTS, N_CP, 8, 128), jnp.float32),
                pltpu.VMEM((N_SLOTS, N_GROUPS, N_HALF, G_ROWS, HD), jnp.float32),
                pltpu.VMEM((N_SLOTS, N_GROUPS, N_CP, G_ROWS, HD), jnp.float32),
                pltpu.VMEM((N_SLOTS, N_GROUPS, N_HALF, G_ROWS, HD), jnp.bfloat16),
                pltpu.VMEM((N_SLOTS, 2, N_HALF, K_LOCAL, HD), jnp.float32),
                pltpu.SemaphoreType.DMA((N_SLOTS, 3)),
                pltpu.SemaphoreType.DMA((N_SLOTS, 3, N_CP)),
                pltpu.SemaphoreType.DMA((N_SLOTS, 2, N_HALF)),
                pltpu.SemaphoreType.DMA((2, N_SLOTS)),
                pltpu.SemaphoreType.DMA((2,)),
            ],
            compiler_params=pltpu.CompilerParams(collective_id=0, has_side_effects=True, vmem_limit_bytes=40 * 1024 * 1024),
            name="head_exchange",
        )(qd, kv, stats)

        dq = dq.reshape(N_HEADS, rows, HD).transpose(1, 0, 2).reshape(queries.shape)
        return dq, dkv[:, 0].transpose(1, 0, 2), dkv[:, 1].transpose(1, 0, 2)

    return jax.shard_map(per_device, mesh=mesh, in_specs=(spec_q, spec_kv, spec_kv, spec_q, spec_lse, spec_q), out_specs=(spec_q, spec_kv, spec_kv), check_vma=False)
```

time: 176 us -> 139 us (0.79); the launches traced: 174 us -> 139 us
  Pallas kernels: 166 us -> 131 us
    pallas_call x1, Pallas kernels: 166 us -> 131 us  [per_device(): pl.pallas_call(kernel, out_shape=(jax.ShapeDtypeStruct((N_HEADS, N_GROUPS...]
where the time goes in v2:
time: 139 us
  Pallas kernels  131 us (94%)
  local copies, waits for them, and re-layouts  5.32 us (4%)
  other arithmetic  2.04 us (1%)
    pallas_call x1, Pallas kernels, per_device(): pl.pallas_call(kernel, out_shape=(jax.ShapeDtypeStruct((N_HEADS, N_GROUPS...  131 us

profile of v2, /device:TPU:0, one launch (start us, length us, event | category | flops | bytes accessed | tf_op | source)
XLA Modules:
  0.0 139.0 jit_solution(8011397197924680094)
XLA Ops:
  0.6 0.0 copy-start.4
  0.6 0.0 copy-start.3
  0.7 0.1 broadcast_in_dim.29
  0.7 0.1 broadcast_in_dim.30
  0.8 1.7 %multiply_reduce_fusion = f32[12,8,26]{1,2,0:T(8,128)S(1)} fusion(bf16[12,8,26,128]{3,1,2,0:T(8,128)(2,1)} %param.9, bf16[12,8,26,128]{3,1,2,0:T(8,128)(2,1)} %param.11), kind=kLoop, calls=%fused_computation.4 | loop fusion | flops 1275456 | bytes 1287936 | tf_op jit(solution)/shard_map/reduce_sum | solution.py:260
  2.5 0.0 copy-start
  2.5 0.1 copy.22
  2.7 0.0 copy-done.4
  2.7 0.1 copy.23
  2.8 0.1 broadcast_in_dim.33
  2.9 0.2 broadcast_in_dim.34
  3.1 0.1 copy_select_fusion
  3.2 0.0 copy-done.3
  3.2 0.1 copy.20
  3.3 0.3 copy-done
  3.6 0.0 copy-start.1
  3.6 0.0 copy-start.2
  3.6 0.1 copy.21
  3.7 0.1 pad_maximum_fusion.1.qd_ref
  3.9 0.9 copy-done.1
  4.8 0.3 copy-done.2
  5.0 0.2 pad_maximum_fusion.kv_ref
  5.2 130.9 %head_exchange.1 = (bf16[26,3,32,128]{3,2,1,0:T(8,128)(2,1)S(1)}, f32[26,2,128,128]{3,2,1,0:T(8,128)S(1)}) custom-call(bf16[26,2,3,32,128]{4,3,2,1,0:T(8,128)(2,1)S(1)} %pad_maximum_fusion.1.qd_ref, bf16[26,2,128,128]{3,2,1,0:T(8,128)(2,1)S(1)} %pad_maximum_fusion.kv_ref, f32[26,8,128]{2,1,0:T(8,128)S(1)} %pad.4.st_ref), custom_call_target="tpu_custom_call" | custom-call | tf_op jit(solution)/shard_map/head_exchange/pallas_call | solution.py:270
  136.1 0.9 copy.25
  137.0 2.0 %slice_bitcast_fusion = (f32[128,26,128]{2,0,1:T(8,128)}, f32[128,26,128]{2,0,1:T(8,128)}) fusion(f32[26,2,128,128]{3,2,1,0:T(8,128)S(1)} %get-tuple-element.6), kind=kLoop, calls=%fused_computation.1 | loop fusion | bytes 6815744 | tf_op jit(solution)/shard_map/transpose | solution.py:297
  (3 shorter events, 0.0 us)
Async XLA Ops:
  0.6 2.1 %copy-start.4 = (f32[12,8,26]{2,1,0:T(8,128)S(1)}, f32[12,8,26]{2,1,0:T(8,128)}, u32[]{:S(2)}) copy-start(f32[12,8,26]{2,1,0:T(8,128)} %param.10) | copy-start | bytes 29956
  0.6 2.5 %copy-start.3 = (bf16[12,8,26,128]{3,1,2,0:T(8,128)(2,1)S(1)}, bf16[12,8,26,128]{3,1,2,0:T(8,128)(2,1)}, u32[]{:S(2)}) copy-start(bf16[12,8,26,128]{3,1,2,0:T(8,128)(2,1)} %param.6) | copy-start | bytes 1916932
  2.5 1.1 copy-start
  3.6 1.2 copy-start.1
  3.6 1.4 %copy-start.2 = (bf16[128,26,128]{2,0,1:T(8,128)(2,1)S(1)}, bf16[128,26,128]{2,0,1:T(8,128)(2,1)}, u32[]{:S(2)}) copy-start(bf16[128,26,128]{2,0,1:T(8,128)(2,1)} %param.7) | copy-start | bytes 2555908

commit v3 on v2

--- a/solution.py
+++ b/solution.py
@@ -11,7 +11,7 @@
 N_CP = 16
 N_HEADS = 26
 N_HALF = 8
-N_SLOTS = 5
+N_SLOTS = 6
 N_GROUPS = 3
 G_ROWS = 32
 SEG_PER_G = 4
@@ -32,15 +32,15 @@
 
 
 def head_of(slot, dev):
-    return jnp.where(at_end(dev), 19 + 3 * slot, 4 * slot) + dev % 4
+    pos = dev % 4
+    return jnp.where(at_end(dev), 22 + pos, jnp.where(slot == 5, 20 + pos // 2, 4 * slot + pos))
 
 
 def slots_of(dev):
-    pos = dev % 4
-    return jnp.where(at_end(dev), jnp.where(pos >= 1, 2, 1), jnp.where(pos <= 2, 5, 4))
-
-
-def kernel(qd_ref, kv_ref, st_ref, dq_out, dkv_out, q_buf, kv_buf, st_buf, part_buf, dq_acc, dq_stage, dkv_stage, in_sems, send_sems, ret_sems, part_sems, out_sems):
+    return jnp.where(at_end(dev), 1, jnp.where(dev % 2 == 0, 6, 5))
+
+
+def kernel(qd_ref, kv_ref, st_ref, dq_out, dkv_out, q_buf, kv_buf, st_buf, part_buf, dq_acc, dq_stage, dkv_stage, in_sems, send_sems, direct_sems, fwd_sems, ret_sems, part_sems, out_sems):
     me = lax.axis_index("cp")
     my_slots = slots_of(me)
     half = me // N_HALF
@@ -57,47 +57,95 @@
     lax.fori_loop(1, N_CP, greet, 0)
     pl.semaphore_wait(barrier, N_CP - 1)
 
-    def in_parts(slot, dev, dev_half):
+    def in_parts(slot, dev):
         head = head_of(slot, dev)
-        first = dev_half
-        q_part = (0, qd_ref.at[head, :, first:], q_buf.at[slot, :, first:, me])
-        kv_part = (1, kv_ref.at[head], kv_buf.at[slot, :, me % N_HALF])
-        st_part = (2, st_ref.at[head], st_buf.at[slot, me])
-        return q_part, kv_part, st_part
-
-    def in_remote(slot, dev, part):
-        kind, src, dst = part
-        return pltpu.make_async_remote_copy(
-            src_ref=src, dst_ref=dst, send_sem=send_sems.at[slot, kind, dev], recv_sem=in_sems.at[slot, kind],
-            device_id={"cp": dev}, device_id_type=MESH,
+        return (
+            (0, qd_ref.at[head], q_buf.at[slot, :, :, me]),
+            (1, kv_ref.at[head], kv_buf.at[slot, :, me % N_HALF]),
+            (2, st_ref.at[head], st_buf.at[slot, me]),
         )
 
-    def each_in_copy(slot, dev, act):
-        for dev_half in range(2):
-
-            @pl.when((slot < slots_of(dev)) & (dev // N_HALF == dev_half))
-            def _():
-                q_part, kv_part, st_part = in_parts(slot, dev, dev_half)
-                act(in_remote(slot, dev, st_part))
-                act(in_remote(slot, dev, q_part))
-
-                @pl.when(half == dev_half)
-                def _():
-                    act(in_remote(slot, dev, kv_part))
+    def each_in_copy(slot, act):
+        def one(k, carry):
+            dev = half_dev + lax.rem(me + k, N_HALF)
+
+            @pl.when(slot < slots_of(dev))
+            def _():
+                for kind, src, dst in in_parts(slot, dev):
+                    act(pltpu.make_async_remote_copy(
+                        src_ref=src, dst_ref=dst, send_sem=send_sems.at[slot, kind, dev % N_HALF], recv_sem=in_sems.at[slot, kind],
+                        device_id={"cp": dev}, device_id_type=MESH,
+                    ))
+
+            return carry
+
+        lax.fori_loop(1, N_HALF, one, 0)
+
+    def each_direct_copy(act):
+        for my_half in range(2):
+
+            @pl.when(half == my_half)
+            def _():
+                first = 1 - my_half
+
+                def one(k, carry):
+                    dev = (1 - my_half) * N_HALF + lax.rem(me + k, N_HALF)
+                    head = head_of(0, dev)
+                    parts = ((qd_ref.at[head, :, first:], q_buf.at[0, :, first:, me]), (st_ref.at[head], st_buf.at[0, me]))
+                    for kind, (src, dst) in enumerate(parts):
+                        act(pltpu.make_async_remote_copy(
+                            src_ref=src, dst_ref=dst, send_sem=direct_sems.at[kind, dev % N_HALF], recv_sem=fwd_sems.at[1, 0, kind],
+                            device_id={"cp": dev}, device_id_type=MESH,
+                        ))
+                    return carry
+
+                lax.fori_loop(0, N_HALF, one, 0)
 
     for slot in range(N_SLOTS):
-        for my_half in range(2):
-
-            @pl.when((slot < my_slots) & (half == my_half))
-            def _():
-                for kind, src, dst in in_parts(slot, me, my_half):
-                    pltpu.make_async_copy(src, dst, in_sems.at[slot, kind]).start()
-
-        def send(k, carry):
-            each_in_copy(slot, lax.rem(me + k, N_CP), lambda copy: copy.start())
-            return carry
-
-        lax.fori_loop(1, N_CP, send, 0)
+
+        @pl.when(slot < my_slots)
+        def _():
+            for kind, src, dst in in_parts(slot, me):
+                pltpu.make_async_copy(src, dst, in_sems.at[slot, kind]).start()
+
+        if slot == 0:
+            each_direct_copy(lambda copy: copy.start())
+        each_in_copy(slot, lambda copy: copy.start())
+
+    def slab(slot, of_half):
+        first = 1 - of_half
+        return q_buf.at[slot, :, first:, of_half * N_HALF:(of_half + 1) * N_HALF]
+
+    def stat_slab(slot, of_half):
+        return st_buf.at[slot, of_half * N_HALF:(of_half + 1) * N_HALF]
+
+    def forwards(slot, my_half):
+        return [
+            pltpu.make_async_remote_copy(
+                src_ref=ref, dst_ref=ref, send_sem=fwd_sems.at[0, slot, kind], recv_sem=fwd_sems.at[1, slot, kind],
+                device_id={"cp": partner}, device_id_type=MESH,
+            )
+            for kind, ref in enumerate((slab(slot, my_half), stat_slab(slot, my_half)))
+        ]
+
+    def receive(slot):
+        own = pl.ds(half_dev, N_HALF)
+        for kind, ref in enumerate((q_buf.at[slot, :, :, own], kv_buf.at[slot], st_buf.at[slot, own])):
+            pltpu.make_async_copy(ref, ref, in_sems.at[slot, kind]).wait()
+        for my_half in range(2):
+
+            @pl.when((half == my_half) & (slot > 0))
+            def _():
+                for copy in forwards(slot, my_half):
+                    copy.start()
+
+    def receive_forwarded(slot):
+        for my_half in range(2):
+
+            @pl.when(half == my_half)
+            def _():
+                for kind, ref in enumerate((slab(slot, 1 - my_half), stat_slab(slot, 1 - my_half))):
+                    pltpu.make_async_copy(ref, ref, fwd_sems.at[1, slot, kind]).wait()
 
     def dkv_remote(slot, dev):
         return pltpu.make_async_remote_copy(
@@ -144,15 +192,11 @@
         lax.fori_loop(1, N_HALF, give_dq, 0)
 
     def run_slot(slot, carry):
-        for my_half in range(2):
-
-            @pl.when(half == my_half)
-            def _():
-                arrived = q_buf.at[slot, :, my_half:]
-                pltpu.make_async_copy(arrived, arrived, in_sems.at[slot, 0]).wait()
-
-        for kind, buf in ((1, kv_buf), (2, st_buf)):
-            pltpu.make_async_copy(buf.at[slot], buf.at[slot], in_sems.at[slot, kind]).wait()
+        @pl.when((slot > 0) & (slot + 1 < my_slots))
+        def _():
+            receive(slot + 1)
+
+        receive_forwarded(slot)
         dq_acc[slot] = jnp.zeros(dq_acc.shape[1:], jnp.float32)
 
         def run_super(sup_local, carry):
@@ -214,40 +258,45 @@
             def _():
                 part_remote(slot, my_half).start()
 
+        @pl.when((slot == 0) & (my_slots > 1))
+        def _():
+            receive(slot + 1)
+
         @pl.when(slot > 0)
         def _():
             finish_dq(slot - 1)
 
         return carry
 
+    receive(0)
     lax.fori_loop(0, my_slots, run_slot, 0)
     finish_dq(my_slots - 1)
 
-    pltpu.make_async_copy(dq_out, dq_out, out_sems.at[0]).wait()
-    pltpu.make_async_copy(dkv_out, dkv_out, out_sems.at[1]).wait()
-
     for slot in range(N_SLOTS):
-
-        def drain(k, carry):
-            each_in_copy(slot, lax.rem(me + k, N_CP), lambda copy: copy.wait_send())
-            return carry
-
-        lax.fori_loop(1, N_CP, drain, 0)
+        each_in_copy(slot, lambda copy: copy.wait_send())
+        if slot == 0:
+            each_direct_copy(lambda copy: copy.wait_send())
 
         @pl.when(slot < my_slots)
         def _():
-            def drain_back(k, carry):
+            def drain(k, carry):
                 dev = half_dev + lax.rem(me + k, N_HALF)
                 dq_remote(slot, dev).wait_send()
                 dkv_remote(slot, dev).wait_send()
                 return carry
 
-            lax.fori_loop(1, N_HALF, drain_back, 0)
+            lax.fori_loop(1, N_HALF, drain, 0)
             for my_half in range(2):
 
                 @pl.when(half == my_half)
                 def _():
+                    if slot > 0:
+                        for copy in forwards(slot, my_half):
+                            copy.wait_send()
                     part_remote(slot, my_half).wait_send()
+
+    pltpu.make_async_copy(dq_out, dq_out, out_sems.at[0]).wait()
+    pltpu.make_async_copy(dkv_out, dkv_out, out_sems.at[1]).wait()
 
 
 def solution(mesh):
@@ -284,7 +333,9 @@
                 pltpu.VMEM((N_SLOTS, N_GROUPS, N_HALF, G_ROWS, HD), jnp.bfloat16),
                 pltpu.VMEM((N_SLOTS, 2, N_HALF, K_LOCAL, HD), jnp.float32),
                 pltpu.SemaphoreType.DMA((N_SLOTS, 3)),
-                pltpu.SemaphoreType.DMA((N_SLOTS, 3, N_CP)),
+                pltpu.SemaphoreType.DMA((N_SLOTS, 3, N_HALF)),
+                pltpu.SemaphoreType.DMA((2, N_HALF)),
+                pltpu.SemaphoreType.DMA((2, N_SLOTS, 2)),
                 pltpu.SemaphoreType.DMA((N_SLOTS, 2, N_HALF)),
                 pltpu.SemaphoreType.DMA((2, N_SLOTS)),
                 pltpu.SemaphoreType.DMA((2,)),

time: 139 us -> 132 us (0.950); the launches traced: 139 us -> 130 us
  Pallas kernels: 131 us -> 122 us
    pallas_call x1, Pallas kernels: 131 us -> 122 us  [per_device(): pl.pallas_call(kernel, out_shape=(jax.ShapeDtypeStruct((N_HEADS, N_GROUPS...]
where the time goes in v3:
time: 132 us; the launch traced here: 130 us
  Pallas kernels  122 us (92%)
  local copies, waits for them, and re-layouts  5.32 us (4%)
  other arithmetic  2.04 us (2%)
    pallas_call x1, Pallas kernels, per_device(): pl.pallas_call(kernel, out_shape=(jax.ShapeDtypeStruct((N_HEADS, N_GROUPS...  122 us
    unnamed x13, local copies, waits for them, and re-layouts  2.68 us

profile of v3, /device:TPU:0, one launch (start us, length us, event | category | flops | bytes accessed | tf_op | source)
XLA Modules:
  0.0 130.2 jit_solution(3973476818144441065)
XLA Ops:
  0.6 0.0 copy-start.4
  0.6 0.0 copy-start.3
  0.7 0.1 broadcast_in_dim.29
  0.7 0.1 broadcast_in_dim.30
  0.8 1.7 %multiply_reduce_fusion = f32[12,8,26]{1,2,0:T(8,128)S(1)} fusion(bf16[12,8,26,128]{3,1,2,0:T(8,128)(2,1)} %param.9, bf16[12,8,26,128]{3,1,2,0:T(8,128)(2,1)} %param.11), kind=kLoop, calls=%fused_computation.4 | loop fusion | flops 1275456 | bytes 1287936 | tf_op jit(solution)/shard_map/reduce_sum | solution.py:309
  2.5 0.0 copy-start
  2.5 0.1 copy.22
  2.7 0.0 copy-done.4
  2.7 0.1 copy.23
  2.8 0.1 broadcast_in_dim.33
  2.9 0.2 broadcast_in_dim.34
  3.1 0.1 copy_select_fusion
  3.2 0.0 copy-done.3
  3.2 0.1 copy.20
  3.3 0.3 copy-done
  3.6 0.0 copy-start.1
  3.6 0.0 copy-start.2
  3.6 0.1 copy.21
  3.7 0.1 pad_maximum_fusion.1.qd_ref
  3.9 0.9 copy-done.1
  4.8 0.3 copy-done.2
  5.0 0.2 pad_maximum_fusion.kv_ref
  5.2 122.1 %head_exchange.1 = (bf16[26,3,32,128]{3,2,1,0:T(8,128)(2,1)S(1)}, f32[26,2,128,128]{3,2,1,0:T(8,128)S(1)}) custom-call(bf16[26,2,3,32,128]{4,3,2,1,0:T(8,128)(2,1)S(1)} %pad_maximum_fusion.1.qd_ref, bf16[26,2,128,128]{3,2,1,0:T(8,128)(2,1)S(1)} %pad_maximum_fusion.kv_ref, f32[26,8,128]{2,1,0:T(8,128)S(1)} %pad.4.st_ref), custom_call_target="tpu_custom_call" | custom-call | tf_op jit(solution)/shard_map/head_exchange/pallas_call | solution.py:319
  127.3 0.9 copy.25
  128.2 2.0 %slice_bitcast_fusion = (f32[128,26,128]{2,0,1:T(8,128)}, f32[128,26,128]{2,0,1:T(8,128)}) fusion(f32[26,2,128,128]{3,2,1,0:T(8,128)S(1)} %get-tuple-element.6), kind=kLoop, calls=%fused_computation.1 | loop fusion | bytes 6815744 | tf_op jit(solution)/shard_map/transpose | solution.py:348
  (3 shorter events, 0.0 us)
Async XLA Ops:
  0.6 2.1 %copy-start.4 = (f32[12,8,26]{2,1,0:T(8,128)S(1)}, f32[12,8,26]{2,1,0:T(8,128)}, u32[]{:S(2)}) copy-start(f32[12,8,26]{2,1,0:T(8,128)} %param.10) | copy-start | bytes 29956
  0.6 2.5 %copy-start.3 = (bf16[12,8,26,128]{3,1,2,0:T(8,128)(2,1)S(1)}, bf16[12,8,26,128]{3,1,2,0:T(8,128)(2,1)}, u32[]{:S(2)}) copy-start(bf16[12,8,26,128]{3,1,2,0:T(8,128)(2,1)} %param.6) | copy-start | bytes 1916932
  2.5 1.1 copy-start
  3.6 1.2 copy-start.1
  3.6 1.4 %copy-start.2 = (bf16[128,26,128]{2,0,1:T(8,128)(2,1)S(1)}, bf16[128,26,128]{2,0,1:T(8,128)(2,1)}, u32[]{:S(2)}) copy-start(bf16[128,26,128]{2,0,1:T(8,128)(2,1)} %param.7) | copy-start | bytes 2555908

commit v4 on v3

--- a/solution.py
+++ b/solution.py
@@ -66,20 +66,23 @@
         )
 
     def each_in_copy(slot, act):
-        def one(k, carry):
-            dev = half_dev + lax.rem(me + k, N_HALF)
-
-            @pl.when(slot < slots_of(dev))
-            def _():
-                for kind, src, dst in in_parts(slot, dev):
-                    act(pltpu.make_async_remote_copy(
-                        src_ref=src, dst_ref=dst, send_sem=send_sems.at[slot, kind, dev % N_HALF], recv_sem=in_sems.at[slot, kind],
-                        device_id={"cp": dev}, device_id_type=MESH,
-                    ))
-
-            return carry
-
-        lax.fori_loop(1, N_HALF, one, 0)
+        for kinds in ((0, 2), (1,)):
+
+            def one(n, carry):
+                dev = half_dev + lax.rem(me + n, N_HALF)
+
+                @pl.when(slot < slots_of(dev))
+                def _():
+                    parts = in_parts(slot, dev)
+                    for kind in kinds:
+                        act(pltpu.make_async_remote_copy(
+                            src_ref=parts[kind][1], dst_ref=parts[kind][2], send_sem=send_sems.at[slot, kind, dev % N_HALF],
+                            recv_sem=in_sems.at[slot, kind], device_id={"cp": dev}, device_id_type=MESH,
+                        ))
+
+                return carry
+
+            lax.fori_loop(1, N_HALF, one, 0)
 
     def each_direct_copy(act):
         for my_half in range(2):
@@ -130,7 +133,7 @@
 
     def receive(slot):
         own = pl.ds(half_dev, N_HALF)
-        for kind, ref in enumerate((q_buf.at[slot, :, :, own], kv_buf.at[slot], st_buf.at[slot, own])):
+        for kind, ref in ((0, q_buf.at[slot, :, :, own]), (2, st_buf.at[slot, own])):
             pltpu.make_async_copy(ref, ref, in_sems.at[slot, kind]).wait()
         for my_half in range(2):
 
@@ -197,6 +200,7 @@
             receive(slot + 1)
 
         receive_forwarded(slot)
+        pltpu.make_async_copy(kv_buf.at[slot], kv_buf.at[slot], in_sems.at[slot, 1]).wait()
         dq_acc[slot] = jnp.zeros(dq_acc.shape[1:], jnp.float32)
 
         def run_super(sup_local, carry):

time: 132 us -> 133 us (level)
  no operation moved by 1% of the time
where the time goes in v4:
time: 133 us; the launch traced here: 131 us
  Pallas kernels  123 us (92%)
  local copies, waits for them, and re-layouts  5.32 us (4%)
  other arithmetic  2.04 us (2%)
    pallas_call x1, Pallas kernels, per_device(): pl.pallas_call(kernel, out_shape=(jax.ShapeDtypeStruct((N_HEADS, N_GROUPS...  123 us
    unnamed x13, local copies, waits for them, and re-layouts  2.68 us

profile of v4, /device:TPU:0, one launch (start us, length us, event | category | flops | bytes accessed | tf_op | source)
XLA Modules:
  0.0 131.1 jit_solution(12612765993089411290)
XLA Ops:
  0.6 0.0 copy-start.4
  0.6 0.0 copy-start.3
  0.7 0.1 broadcast_in_dim.29
  0.7 0.1 broadcast_in_dim.30
  0.8 1.7 %multiply_reduce_fusion = f32[12,8,26]{1,2,0:T(8,128)S(1)} fusion(bf16[12,8,26,128]{3,1,2,0:T(8,128)(2,1)} %param.9, bf16[12,8,26,128]{3,1,2,0:T(8,128)(2,1)} %param.11), kind=kLoop, calls=%fused_computation.4 | loop fusion | flops 1275456 | bytes 1287936 | tf_op jit(solution)/shard_map/reduce_sum | solution.py:313
  2.5 0.0 copy-start
  2.5 0.1 copy.22
  2.7 0.0 copy-done.4
  2.7 0.1 copy.23
  2.8 0.1 broadcast_in_dim.33
  2.9 0.2 broadcast_in_dim.34
  3.1 0.1 copy_select_fusion
  3.2 0.0 copy-done.3
  3.2 0.1 copy.20
  3.3 0.3 copy-done
  3.6 0.0 copy-start.1
  3.6 0.0 copy-start.2
  3.6 0.1 copy.21
  3.7 0.1 pad_maximum_fusion.1.qd_ref
  3.9 0.9 copy-done.1
  4.8 0.3 copy-done.2
  5.0 0.2 pad_maximum_fusion.kv_ref
  5.2 122.9 %head_exchange.1 = (bf16[26,3,32,128]{3,2,1,0:T(8,128)(2,1)S(1)}, f32[26,2,128,128]{3,2,1,0:T(8,128)S(1)}) custom-call(bf16[26,2,3,32,128]{4,3,2,1,0:T(8,128)(2,1)S(1)} %pad_maximum_fusion.1.qd_ref, bf16[26,2,128,128]{3,2,1,0:T(8,128)(2,1)S(1)} %pad_maximum_fusion.kv_ref, f32[26,8,128]{2,1,0:T(8,128)S(1)} %pad.4.st_ref), custom_call_target="tpu_custom_call" | custom-call | tf_op jit(solution)/shard_map/head_exchange/pallas_call | solution.py:323
  128.1 0.9 copy.25
  129.1 2.0 %slice_bitcast_fusion = (f32[128,26,128]{2,0,1:T(8,128)}, f32[128,26,128]{2,0,1:T(8,128)}) fusion(f32[26,2,128,128]{3,2,1,0:T(8,128)S(1)} %get-tuple-element.6), kind=kLoop, calls=%fused_computation.1 | loop fusion | bytes 6815744 | tf_op jit(solution)/shard_map/transpose | solution.py:352
  (3 shorter events, 0.0 us)
Async XLA Ops:
  0.6 2.1 %copy-start.4 = (f32[12,8,26]{2,1,0:T(8,128)S(1)}, f32[12,8,26]{2,1,0:T(8,128)}, u32[]{:S(2)}) copy-start(f32[12,8,26]{2,1,0:T(8,128)} %param.10) | copy-start | bytes 29956
  0.6 2.5 %copy-start.3 = (bf16[12,8,26,128]{3,1,2,0:T(8,128)(2,1)S(1)}, bf16[12,8,26,128]{3,1,2,0:T(8,128)(2,1)}, u32[]{:S(2)}) copy-start(bf16[12,8,26,128]{3,1,2,0:T(8,128)(2,1)} %param.6) | copy-start | bytes 1916932
  2.5 1.1 copy-start
  3.6 1.2 copy-start.1
  3.6 1.4 %copy-start.2 = (bf16[128,26,128]{2,0,1:T(8,128)(2,1)S(1)}, bf16[128,26,128]{2,0,1:T(8,128)(2,1)}, u32[]{:S(2)}) copy-start(bf16[128,26,128]{2,0,1:T(8,128)(2,1)} %param.7) | copy-start | bytes 2555908
